TPU v7x, 256 devices: a whole 4x4x8 slice. The times are simulated.
256 devices in a mesh: expert: 8 (over y_lo, x), rep: 32 (over z, y_hi, core).
Axes of the slice: x: 4, y: 4 (y_hi: 2, y_lo: 2; y = y_hi * 2 + y_lo), z: 8, core: 2. Of those that a mesh axis runs over, the one named last changes fastest.
Arguments:
- route_ids: int32 [2048, 2], P(('expert', 'rep')), may hold values from 0 to 7, all different within a row; in each aligned block of 8 rows (0 to 7, 8 to 15, ...) at most 4 rows name the same one
- route_weight: float32 [2048, 2], P(('expert', 'rep')), may hold values from 0.2 to 0.8
- input_float: bfloat16 [2048, 4096], P(('expert', 'rep')), may hold values from -6 to 6
- input_quant: bfloat16 [2048, 4096], P(('expert', 'rep')), may hold values from -6 to 6
- keep_mask: int32 [2048, 4096], P(('expert', 'rep')), may hold values 0 or 1
- grad_mixed: bfloat16 [2048, 4096], P(('expert', 'rep')), may hold values from -192 to 192
- gate_weight: bfloat16 [8, 4096, 7168], P('expert', None, 'rep'), may hold values from -0.09375 to 0.09375
- up_weight: bfloat16 [8, 4096, 7168], P('expert', None, 'rep'), may hold values from -0.09375 to 0.09375
- down_base: bfloat16 [8, 7168, 4096], P('expert', 'rep'), may hold values from -0.0625 to 0.0625
- down_round: bfloat16 [8, 7168, 4096], P('expert', 'rep'), may hold values from -8 to 8
- down_step: float32 [8, 4096], P('expert'), may hold values from 0.004 to 0.04
Outputs:
- mixed: bfloat16 [2048, 4096], P(('expert', 'rep'))
- round_grad: float32 [8, 7168, 4096], P('expert', 'rep')
Inputs may be any that keep to these rules, and one draw needn't show every extreme that they name: `route_ids`: within the 8 tokens of one device, each expert is named by at most 4 pairs; the two experts of a token differ.
All inputs are finite; a program needn't handle non-finite values. No bound on the sum of `keep_mask` on one device may be relied on, other than what follows from the above.
Results may differ from a plain program's by a relative error of at most 0.0065.
Values may be sent and summed in bfloat16 or wider, within the bound.
No kernel may reach another device: no remote copies, remote signals or barrier semaphores. Data moves between devices by JAX's collectives and lax.ppermute only.
A program may use at most 128 MiB of HBM per device.

v0:
```python
import jax
import jax.numpy as jnp
from jax import lax
from jax.sharding import PartitionSpec as P


def in_one_piece(arrays, axis, split_dim, concat_dim, along):
    both = jnp.concatenate(arrays, axis=along)
    filled, at, gathered = (
        lax.all_to_all(both, axis, split_axis=split_dim, concat_axis=concat_dim, tiled=True),
        0,
        [],
    )
    for a in arrays:
        gathered.append(lax.slice_in_dim(filled, at, at + a.shape[along], axis=along))
        at += a.shape[along]
    return tuple(gathered)


def sent_together(arrays, axis, dim, along):
    ends, at = ([], 0)
    for a in arrays[:-1]:
        at += a.shape[along]
        ends.append(at)
    both = jnp.concatenate(arrays, axis=along)
    return tuple(jnp.split(lax.all_gather(both, axis, axis=dim, tiled=True), ends, axis=along))


def local_slots(route_ids, experts):
    count = route_ids.shape[0]
    flat = route_ids.reshape(count * 2)
    onehot = (flat[:, None] == jnp.arange(experts, dtype=jnp.int32)[None, :]).astype(jnp.int32)
    before = jnp.cumsum(onehot, axis=0) - onehot
    return jnp.sum(before * onehot, axis=1).reshape(count, 2)


def body(
    route_ids,
    route_weight,
    input_float,
    input_quant,
    keep_mask,
    grad_mixed,
    gate_weight,
    up_weight,
    down_base,
    down_round,
    down_step,
):
    experts = lax.axis_size("expert")
    count = route_ids.shape[0]
    capacity = count // 2
    slot = local_slots(route_ids, experts)
    target = route_ids * capacity + slot
    columns = jnp.arange(experts * capacity, dtype=jnp.int32)
    first = (target[:, 0:1] == columns[None, :]).astype(jnp.float32)
    second = (target[:, 1:2] == columns[None, :]).astype(jnp.float32)
    placing = (first + second).astype(jnp.bfloat16)
    weighting = route_weight[:, 0:1] * first + route_weight[:, 1:2] * second
    x_in = jnp.where(keep_mask == 1, input_quant, input_float)
    send_rows = lax.dot_general(
        placing, x_in, (((0,), (0,)), ((), ())), preferred_element_type=jnp.float32
    ).astype(jnp.bfloat16)
    send_cot = lax.dot_general(
        weighting,
        grad_mixed.astype(jnp.float32),
        (((0,), (0,)), ((), ())),
        precision=lax.Precision.HIGHEST,
        preferred_element_type=jnp.float32,
    ).astype(jnp.bfloat16)
    own_rows, own_cot = in_one_piece((send_rows, send_cot), "expert", 0, 0, 1)
    w_gate = gate_weight[0]
    w_up = up_weight[0]
    soft = jax.nn.sigmoid(down_round[0].astype(jnp.float32))
    step_row = down_step[0][None, :]
    quant_down = (down_base[0].astype(jnp.float32) + step_row * soft).astype(jnp.bfloat16)
    all_rows, all_cot = sent_together((own_rows, own_cot), "rep", 0, 1)
    gate = jnp.dot(all_rows, w_gate, preferred_element_type=jnp.float32)
    up = jnp.dot(all_rows, w_up, preferred_element_type=jnp.float32)
    hidden = (jax.nn.silu(gate) * up).astype(jnp.bfloat16)
    grad_w = lax.dot_general(
        hidden, all_cot, (((0,), (0,)), ((), ())), preferred_element_type=jnp.float32
    )
    wide_down = lax.all_to_all(quant_down, "rep", split_axis=1, concat_axis=0, tiled=True)
    out_cols = jnp.dot(
        lax.all_gather(hidden, "rep", axis=1, tiled=True),
        wide_down,
        preferred_element_type=jnp.float32,
    )
    summed = lax.all_to_all(
        out_cols.astype(jnp.bfloat16), "rep", split_axis=0, concat_axis=1, tiled=True
    )
    returned = lax.all_to_all(summed, "expert", split_axis=0, concat_axis=0, tiled=True)
    mixed = jnp.dot(
        weighting,
        returned.astype(jnp.float32),
        precision=lax.Precision.HIGHEST,
        preferred_element_type=jnp.float32,
    ).astype(jnp.bfloat16)
    round_grad = (grad_w * step_row * soft * (1.0 - soft))[None]
    return (mixed, round_grad)


def solution(mesh):
    return jax.shard_map(
        body,
        mesh=mesh,
        in_specs=(
            P(("expert", "rep"), None),
            P(("expert", "rep"), None),
            P(("expert", "rep"), None),
            P(("expert", "rep"), None),
            P(("expert", "rep"), None),
            P(("expert", "rep"), None),
            P("expert", None, "rep"),
            P("expert", None, "rep"),
            P("expert", "rep", None),
            P("expert", "rep", None),
            P("expert", None),
        ),
        out_specs=(P(("expert", "rep"), None), P("expert", "rep", None)),
        check_vma=False,
    )
```

profile of v0, /device:TPU:1, one launch (start us, length us, event | category | flops | bytes accessed | tf_op | source)
XLA Modules:
  0.0 381.1 jit_solution(1803155560595772534)
XLA Ops:
  7.2 0.8 slice_bitcast_fusion.1
  8.1 0.8 copy.23
  9.5 1.3 convolution_convert_fusion.1
  10.8 1.3 convolution_convert_fusion
  12.3 14.9 %all_to_all.56 = bf16[8,4,8192]{2,1,0:T(4,128)(2,1)S(1)} all-to-all(bf16[8,4,8192]{2,1,0:T(4,128)(2,1)S(1)} %all_to_all.40), channel_id=1, replica_groups=mesh['expert'=8,'rep'=32] {'expert'}, dimensions={0} | all-to-all | bytes 1048576 | tf_op jit(solution)/shard_map/all_to_all | solution.py:10
  27.2 0.9 all_to_all.42
  28.2 139.6 %all-gather.3.cloned.1.call-done = bf16[1024,8192]{1,0:T(8,128)(2,1)} async-done(((bf16[32,8192]{1,0:T(8,128)(2,1)}), bf16[1024,8192]{1,0:T(8,128)(2,1)}) %all-gather.3.cloned.1.call-update) | async-done | bytes 16777232 | tf_op jit(solution)/shard_map/all_gather | solution.py:26
  167.8 6.1 %fusion.4 = f32[1024,224]{0,1:T(8,128)S(1)} fusion(bf16[1024,8192]{1,0:T(8,128)(2,1)} %all-gather.3.cloned.1.call-done, bf16[1,4096,224]{1,2,0:T(8,128)(2,1)S(1)} %copy-done), kind=kOutput, calls=%fused_computation.4 | convolution fusion | flops 1879048192 | bytes 11141120 | tf_op jit(solution)/shard_map/dot_general | solution.py:78
  174.0 2.0 copy-done.6
  176.5 3.5 fusion.28
  180.5 0.6 copy.27
  181.1 0.8 copy-done.3
  182.0 1.0 fusion.22
  182.9 0.6 copy.28
  183.6 0.9 fusion.19
  184.6 0.7 copy.25
  185.3 67.5 %all_to_all.57 = bf16[224,32,128]{2,0,1:T(8,128)(2,1)S(1)} all-to-all(bf16[224,32,128]{2,0,1:T(8,128)(2,1)S(1)} %copy.25), channel_id=1, replica_groups=mesh['expert'=8,'rep'=32] {'rep'}, dimensions={1} | all-to-all | bytes 3670016 | tf_op jit(solution)/shard_map/all_to_all | solution.py:84
  252.8 81.7 %all-gather.5.cloned.1.call-done = bf16[1024,7168]{0,1:T(8,128)(2,1)} async-done(((bf16[1024,224]{0,1:T(8,128)(2,1)}), bf16[1024,7168]{0,1:T(8,128)(2,1)}) %all-gather.5.cloned.1.call-update) | async-done | bytes 14680080 | tf_op jit(solution)/shard_map/all_gather | solution.py:86
  334.5 7.3 %convolution_convert_fusion.3 = bf16[1024,128]{1,0:T(8,128)(2,1)S(1)} fusion(bf16[1024,7168]{0,1:T(8,128)(2,1)} %all-gather.5.cloned.1.call-done, bf16[7168,128]{1,0:T(8,128)(2,1)S(1)} %bitcast.47), kind=kOutput, calls=%fused_computation.24 | convolution fusion | flops 1879179264 | bytes 16777216 | tf_op jit(solution)/shard_map/dot_general | solution.py:85
  341.9 17.4 %all_to_all.58 = bf16[32,32,128]{2,1,0:T(8,128)(2,1)S(1)} all-to-all(bf16[32,32,128]{2,1,0:T(8,128)(2,1)S(1)} %bitcast.49), channel_id=1, replica_groups=mesh['expert'=8,'rep'=32] {'rep'}, dimensions={0} | all-to-all | bytes 524288 | tf_op jit(solution)/shard_map/all_to_all | solution.py:90
  359.4 0.8 all_to_all.49
  360.2 4.8 %all-to-all-start.3 = ((bf16[8,4,4096]{2,1,0:T(4,128)(2,1)}), bf16[8,4,4096]{2,1,0:T(4,128)(2,1)S(1)}, u32[]{:S(2)}, u32[]{:S(2)}) async-start(bf16[8,4,4096]{2,1,0:T(4,128)(2,1)} %all_to_all.49), calls=%async_computation.3 | async-start | bytes 524288 | tf_op jit(solution)/shard_map/all_to_all | solution.py:93
  365.1 8.2 %fusion.15 = f32[1,224,4096]{2,1,0:T(8,128)} fusion(bf16[1024,224]{0,1:T(8,128)(2,1)S(1)} %copy-done.4, bf16[1024,8192]{1,0:T(8,128)(2,1)} %all-gather.3.cloned.1.call-done, f32[4096]{0:T(1024)S(1)} %bitcast.51, bf16[1,224,4096]{2,1,0:T(8,128)(2,1)} %param.20), kind=kOutput, calls=%fused_computation.9 | convolution fusion | flops 1886388224 | bytes 14368768 | tf_op jit(solution)/shard_map/dot_general | solution.py:81
  373.3 0.9 convolution_convert_fusion.2
  (31 shorter events, 2.2 us)
Async XLA Ops:
  7.2 160.7 %copy-start = (bf16[1,4096,224]{1,2,0:T(8,128)(2,1)S(1)}, bf16[1,4096,224]{1,2,0:T(8,128)(2,1)}, u32[]{:S(2)}) copy-start(bf16[1,4096,224]{1,2,0:T(8,128)(2,1)} %param.17) | copy-start | bytes 5505028
  7.2 160.6 %all-gather.3.cloned.1.call-start = ((), (), s32[]{:S(2)}) async-start(), calls=%async_computation.4 | async-start | bytes 17301504 | tf_op jit(solution)/shard_map/all_gather | solution.py:26
  28.2 306.3 %all-gather.5.cloned.1.call-start = ((), (), s32[]{:S(2)}) async-start(), calls=%async_computation.5 | async-start | bytes 15138816 | tf_op jit(solution)/shard_map/all_gather | solution.py:86
  167.8 8.2 %copy-start.6 = (bf16[1024,8192]{1,0:T(8,128)(2,1)S(1)}, bf16[1024,8192]{1,0:T(8,128)(2,1)}, u32[]{:S(2)}) copy-start(bf16[1024,8192]{1,0:T(8,128)(2,1)} %all-gather.3.cloned.1.call-done) | copy-start | bytes 50331652
  167.8 8.7 %copy-start.7 = (bf16[1,4096,224]{1,2,0:T(8,128)(2,1)S(1)}, bf16[1,4096,224]{1,2,0:T(8,128)(2,1)}, u32[]{:S(2)}) copy-start(bf16[1,4096,224]{1,2,0:T(8,128)(2,1)} %param.18) | copy-start | bytes 5505028
  176.5 3.6 copy-start.2
  180.5 1.5 copy-start.3
  182.9 0.7 copy-start.5
  334.5 30.5 %copy-start.4 = (bf16[1024,224]{0,1:T(8,128)(2,1)S(1)}, bf16[1024,224]{0,1:T(8,128)(2,1)}, u32[]{:S(2)}) copy-start(bf16[1024,224]{0,1:T(8,128)(2,1)} %fusion.28) | copy-start | bytes 1376260
  360.2 13.1 %all-to-all-start.3 = ((bf16[8,4,4096]{2,1,0:T(4,128)(2,1)}), bf16[8,4,4096]{2,1,0:T(4,128)(2,1)S(1)}, u32[]{:S(2)}, u32[]{:S(2)}) async-start(bf16[8,4,4096]{2,1,0:T(4,128)(2,1)} %all_to_all.49), calls=%async_computation.3 | async-start | bytes 524288 | tf_op jit(solution)/shard_map/all_to_all | solution.py:93
  365.0 9.2 %copy-start.1 = (bf16[1,4096,224]{1,2,0:T(8,128)(2,1)S(1)}, bf16[1,4096,224]{1,2,0:T(8,128)(2,1)}, u32[]{:S(2)}) copy-start(bf16[1,4096,224]{1,2,0:T(8,128)(2,1)} %param.17) | copy-start | bytes 5505028
Sparse Core Ops, SparseCore 0:
  28.3 139.4 all-gather.2
  180.2 154.3 all-gather.4
where the time goes:
time: 382 us; the launch traced here: 381 us
  waiting for transfers between devices  221 us (58%)
  blocking collectives  99.8 us (26%)
  matrix products  28.8 us (8%)
  between operations  14.2 us (4%)
  local copies, waits for them, and re-layouts  9.41 us (2%)
  starting transfers between devices  4.93 us (1%)
    all_gather x1, waiting for transfers between devices, sent_together(): lax.all_gather(both, axis, axis=dim, tiled=True)  140 us
    all_gather x1, waiting for transfers between devices, body(): lax.all_gather(hidden, 'rep', axis=1, tiled=True)  81.7 us
    all_to_all x1, blocking collectives, body(): lax.all_to_all(quant_down, 'rep', split_axis=1, concat_axis=0, tiled=True)  67.5 us
    all_to_all x1, blocking collectives, body(): lax.all_to_all(out_cols.astype(jnp.bfloat16), 'rep', split_axis=0, concat...  17.4 us
    all_to_all x1, blocking collectives, in_one_piece(): lax.all_to_all(both, axis, split_axis=split_dim, concat_axis=concat_dim,...  14.9 us
    dot_general x1, matrix products, body(): lax.dot_general(hidden, all_cot, (((0,), (0,)), ((), ())), preferred_elem...  8.21 us
  transfers between devices with their start and end apart: 3, of which 2 were waited for; matrix products, arithmetic and copies ran while one was open for 3% of the time, Pallas kernels for 0%

commit v1 on v0

--- a/solution.py
+++ b/solution.py
@@ -83,7 +83,9 @@
     )
     wide_down = lax.all_to_all(quant_down, "rep", split_axis=1, concat_axis=0, tiled=True)
     out_cols = jnp.dot(
-        lax.all_gather(hidden, "rep", axis=1, tiled=True),
+        jnp.concatenate(
+            lax.all_to_all(jnp.stack([hidden] * lax.axis_size("rep")), "rep", 0, 0), axis=1
+        ),
         wide_down,
         preferred_element_type=jnp.float32,
     )

time: 382 us -> 592 us (1.55)
  blocking collectives: 99.8 us -> 358 us
  waiting for transfers between devices: 221 us -> 150 us
  starting transfers between devices: 4.93 us -> 17.7 us
  local copies, waits for them, and re-layouts: 9.41 us -> 15.8 us
  other arithmetic: 2.61 us -> 8.68 us
    all_to_all x1, blocking collectives: 67.5 us -> 325 us  [body(): lax.all_to_all(jnp.stack([hidden] * lax.axis_size('rep')), 'rep', 0, 0)]
    all_gather x1 -> x0, waiting for transfers between devices: 81.7 us -> none  [body(): lax.all_gather(hidden, 'rep', axis=1, tiled=True)]
    all_to_all x0 -> x1, starting transfers between devices: none -> 12.8 us  [body(): lax.all_to_all(quant_down, 'rep', split_axis=1, concat_axis=0, tiled=True)]
    all_gather x1, waiting for transfers between devices: 140 us -> 150 us  [sent_together(): lax.all_gather(both, axis, axis=dim, tiled=True)]
    another operation x0 -> x1, local copies, waits for them, and re-layouts: none -> 7.08 us  [body(): jnp.stack([hidden] * lax.axis_size('rep'))]
  transfers between devices with their start and end apart: 3 -> 3, of which waited for: 2 -> 1; matrix products, arithmetic and copies ran while one was open for 3% -> 5% of each run, Pallas kernels for 0% -> 0%
where the time goes in v1:
time: 592 us; the launch traced here: 591 us
  blocking collectives  358 us (60%)
  waiting for transfers between devices  150 us (25%)
  matrix products  26.2 us (4%)
  starting transfers between devices  17.7 us (3%)
  local copies, waits for them, and re-layouts  15.8 us (3%)
  between operations  14.2 us (2%)
  other arithmetic  8.68 us (1%)
    all_to_all x1, blocking collectives, body(): lax.all_to_all(jnp.stack([hidden] * lax.axis_size('rep')), 'rep', 0, 0)  325 us
    all_gather x1, waiting for transfers between devices, sent_together(): lax.all_gather(both, axis, axis=dim, tiled=True)  150 us
    all_to_all x1, blocking collectives, body(): lax.all_to_all(out_cols.astype(jnp.bfloat16), 'rep', split_axis=0, concat...  18.6 us
    all_to_all x1, blocking collectives, in_one_piece(): lax.all_to_all(both, axis, split_axis=split_dim, concat_axis=concat_dim,...  14.9 us
    all_to_all x1, starting transfers between devices, body(): lax.all_to_all(quant_down, 'rep', split_axis=1, concat_axis=0, tiled=True)  12.8 us
  transfers between devices with their start and end apart: 3, of which 1 were waited for; matrix products, arithmetic and copies ran while one was open for 5% of the time, Pallas kernels for 0%

profile of v1, /device:TPU:1, one launch (start us, length us, event | category | flops | bytes accessed | tf_op | source)
XLA Modules:
  0.0 591.0 jit_solution(10759255446533942004)
XLA Ops:
  7.2 0.8 slice_bitcast_fusion.1
  8.1 0.8 copy.20
  9.5 1.3 convolution_convert_fusion.1
  10.8 1.3 convolution_convert_fusion
  12.3 14.9 %all_to_all.58 = bf16[8,4,8192]{2,1,0:T(4,128)(2,1)S(1)} all-to-all(bf16[8,4,8192]{2,1,0:T(4,128)(2,1)S(1)} %all_to_all.41), channel_id=1, replica_groups=mesh['expert'=8,'rep'=32] {'expert'}, dimensions={0} | all-to-all | bytes 1048576 | tf_op jit(solution)/shard_map/all_to_all | solution.py:10
  27.2 0.9 all_to_all.43
  28.2 1.9 convert_bitcast_fusion
  30.7 0.8 copy-done.2
  31.6 1.0 fusion.24
  32.6 0.6 copy.26
  33.3 5.5 fusion.20
  38.7 12.8 %all-to-all-start.2 = ((bf16[224,32,128]{2,0,1:T(8,128)(2,1)}), bf16[224,32,128]{2,0,1:T(8,128)(2,1)}, u32[]{:S(2)}, u32[]{:S(2)}) async-start(bf16[224,32,128]{2,0,1:T(8,128)(2,1)} %fusion.20), calls=%async_computation.2 | async-start | bytes 3670016 | tf_op jit(solution)/shard_map/all_to_all | solution.py:84
  51.6 150.1 %all-gather.2.cloned.1.call-done = bf16[1024,8192]{1,0:T(8,128)(2,1)} async-done(((bf16[32,8192]{1,0:T(8,128)(2,1)}), bf16[1024,8192]{1,0:T(8,128)(2,1)}) %all-gather.2.cloned.1.call-update) | async-done | bytes 16777232 | tf_op jit(solution)/shard_map/all_gather | solution.py:26
  201.7 6.1 %fusion.6 = f32[1024,224]{0,1:T(8,128)S(1)} fusion(bf16[1024,8192]{1,0:T(8,128)(2,1)} %all-gather.2.cloned.1.call-done, bf16[1,4096,224]{1,2,0:T(8,128)(2,1)S(1)} %copy-done), kind=kOutput, calls=%fused_computation.6 | convolution fusion | flops 1879048192 | bytes 11141120 | tf_op jit(solution)/shard_map/dot_general | solution.py:78
  207.8 2.0 copy-done.4
  210.3 2.7 fusion.30
  213.1 7.1 %stack.2 = bf16[32,1024,224]{1,2,0:T(8,128)(2,1)} broadcast(bf16[1024,224]{0,1:T(8,128)(2,1)S(1)} %fusion.30), dimensions={1,2} | broadcast | bytes 15138816 | tf_op jit(solution)/shard_map/stack | solution.py:87
  220.1 324.9 %all_to_all.59 = bf16[32,1024,224]{1,2,0:T(8,128)(2,1)S(1)} all-to-all(bf16[32,1024,224]{1,2,0:T(8,128)(2,1)} %stack.2), channel_id=1, replica_groups=mesh['expert'=8,'rep'=32] {'rep'}, dimensions={0} | all-to-all | bytes 29360128 | tf_op jit(solution)/shard_map/all_to_all | solution.py:87
  545.0 5.6 fusion.40
  550.6 18.6 %all_to_all.60 = bf16[32,32,128]{2,1,0:T(8,128)(2,1)S(1)} all-to-all(bf16[32,32,128]{2,1,0:T(8,128)(2,1)S(1)} %bitcast.57), channel_id=1, replica_groups=mesh['expert'=8,'rep'=32] {'rep'}, dimensions={0} | all-to-all | bytes 524288 | tf_op jit(solution)/shard_map/all_to_all | solution.py:92
  569.3 0.8 all_to_all.50
  570.1 4.9 all-to-all-start.4
  574.9 8.2 %fusion.17 = f32[1,224,4096]{2,1,0:T(8,128)} fusion(bf16[1024,224]{0,1:T(8,128)(2,1)S(1)} %fusion.30, bf16[1024,8192]{1,0:T(8,128)(2,1)} %all-gather.2.cloned.1.call-done, f32[4096]{0:T(1024)S(1)} %bitcast.59, bf16[1,224,4096]{2,1,0:T(8,128)(2,1)} %param.20), kind=kOutput, calls=%fused_computation.11 | convolution fusion | flops 1886388224 | bytes 14368768 | tf_op jit(solution)/shard_map/dot_general | solution.py:81
  583.2 0.9 convolution_convert_fusion.2
  (26 shorter events, 2.3 us)
Async XLA Ops:
  7.2 194.5 %copy-start = (bf16[1,4096,224]{1,2,0:T(8,128)(2,1)S(1)}, bf16[1,4096,224]{1,2,0:T(8,128)(2,1)}, u32[]{:S(2)}) copy-start(bf16[1,4096,224]{1,2,0:T(8,128)(2,1)} %param.17) | copy-start | bytes 5505028
  7.2 194.5 %all-gather.2.cloned.1.call-start = ((), (), s32[]{:S(2)}) async-start(), calls=%async_computation.5 | async-start | bytes 17301504 | tf_op jit(solution)/shard_map/all_gather | solution.py:26
  30.1 1.5 copy-start.2
  32.5 0.7 copy-start.3
  38.7 174.3 %all-to-all-start.2 = ((bf16[224,32,128]{2,0,1:T(8,128)(2,1)}), bf16[224,32,128]{2,0,1:T(8,128)(2,1)}, u32[]{:S(2)}, u32[]{:S(2)}) async-start(bf16[224,32,128]{2,0,1:T(8,128)(2,1)} %fusion.20), calls=%async_computation.2 | async-start | bytes 3670016 | tf_op jit(solution)/shard_map/all_to_all | solution.py:84
  201.7 8.2 %copy-start.4 = (bf16[1024,8192]{1,0:T(8,128)(2,1)S(1)}, bf16[1024,8192]{1,0:T(8,128)(2,1)}, u32[]{:S(2)}) copy-start(bf16[1024,8192]{1,0:T(8,128)(2,1)} %all-gather.2.cloned.1.call-done) | copy-start | bytes 50331652
  201.7 8.7 %copy-start.5 = (bf16[1,4096,224]{1,2,0:T(8,128)(2,1)S(1)}, bf16[1,4096,224]{1,2,0:T(8,128)(2,1)}, u32[]{:S(2)}) copy-start(bf16[1,4096,224]{1,2,0:T(8,128)(2,1)} %param.18) | copy-start | bytes 5505028
  570.1 13.1 %all-to-all-start.4 = ((bf16[8,4,4096]{2,1,0:T(4,128)(2,1)}), bf16[8,4,4096]{2,1,0:T(4,128)(2,1)S(1)}, u32[]{:S(2)}, u32[]{:S(2)}) async-start(bf16[8,4,4096]{2,1,0:T(4,128)(2,1)} %all_to_all.50), calls=%async_computation.4 | async-start | bytes 524288 | tf_op jit(solution)/shard_map/all_to_all | solution.py:95
  574.9 9.2 %copy-start.1 = (bf16[1,4096,224]{1,2,0:T(8,128)(2,1)S(1)}, bf16[1,4096,224]{1,2,0:T(8,128)(2,1)}, u32[]{:S(2)}) copy-start(bf16[1,4096,224]{1,2,0:T(8,128)(2,1)} %param.17) | copy-start | bytes 5505028
Sparse Core Ops, SparseCore 0:
  28.3 173.3 all-gather.1
